TPU v7x, 32 devices: a whole 2x2x4 slice. The times are simulated.
32 devices in a mesh: fsdp: 16 (over z, x, core), tp: 2 (over y).
Axes of the slice: x: 2, y: 2, z: 4, core: 2. Of those that a mesh axis runs over, the one named last changes fastest.
Arguments:
- hidden: bfloat16 [4096, 8192], P('fsdp'), may hold values from -6 to 6
- norm_gain: float32 [8192], replicated, may hold values from 0.6 to 6, as said below
- w_query: bfloat16 [8192, 4096], P('fsdp', 'tp'), may hold values from -0.09375 to 0.09375
- w_key: bfloat16 [8192, 512], P('fsdp'), may hold values from -0.09375 to 0.09375
- w_value: bfloat16 [8192, 512], P('fsdp'), may hold values from -0.0625 to 0.0625
- bias_query: bfloat16 [4096], P('tp'), may hold values from -3 to 3
- bias_key: bfloat16 [512], replicated, may hold values from -3 to 3
- bias_value: bfloat16 [512], replicated, may hold values from -3 to 3
- w_out: bfloat16 [4096, 8192], P('tp', 'fsdp'), may hold values from -0.09375 to 0.09375
- seq_lengths: int32 [4], replicated, may hold values from 1 to 3072, 4096 in all
Outputs:
- hidden_out: float32 [4096, 8192], P(('fsdp', 'tp'))
Inputs may be any that keep to these rules, and one draw needn't show every extreme that they name: `seq_lengths`: 4 sequences packed in order; the lengths sum to 4096 and the longest has exactly 3072 tokens. `norm_gain`: positive gains.
All inputs are finite; a program needn't handle non-finite values.
Results may differ from a plain program's by a relative error of at most 0.014.
The roundings to bfloat16 on the way count: a program that leaves them out, or rounds other values in their place, can miss the bound.
Values may be sent and summed in bfloat16 or wider, within the bound.
A program may use at most 128 MiB of HBM per device.

v0:
```python
import math
import jax
import jax.numpy as jnp
from jax import lax
from jax.sharding import PartitionSpec as P

HEAD = 128
QHEADS = 32
KVHEADS = 4
ROPE_BASE = 1000000.0
EPSILON = 1e-06
FLOOR = -1e30


def token_layout(seq_lengths, token_index):
    seq_ends = jnp.cumsum(seq_lengths)
    seq_starts = seq_ends - seq_lengths
    member = (token_index[:, None] >= seq_ends[None, :]).astype(jnp.int32)
    segment = jnp.sum(member, axis=1)
    one_hot = segment[:, None] == jnp.arange(seq_lengths.shape[0], dtype=jnp.int32)[None, :]
    seq_begin = jnp.sum(jnp.where(one_hot, seq_starts[None, :], 0), axis=1)
    return (segment, token_index - seq_begin)


def rotary(vectors, position):
    half_size = vectors.shape[-1] // 2
    frequency = jnp.exp(
        jnp.arange(half_size, dtype=jnp.float32) * (-2.0 * math.log(ROPE_BASE) / vectors.shape[-1])
    )
    angle = position.astype(jnp.float32)[:, None] * frequency[None, :]
    cos_table = jnp.concatenate([jnp.cos(angle), jnp.cos(angle)], axis=1)[:, None, :]
    sin_table = jnp.concatenate([jnp.sin(angle), jnp.sin(angle)], axis=1)[:, None, :]
    turned = jnp.concatenate([-vectors[..., half_size:], vectors[..., :half_size]], axis=-1)
    return vectors * cos_table + turned * sin_table


def shards(
    hidden, norm_gain, w_query, w_key, w_value, bias_query, bias_key, bias_value, w_out, seq_lengths
):
    tok_rows = hidden.shape[0]
    first_row = lax.axis_index("fsdp") * tok_rows
    local_index = first_row + jnp.arange(tok_rows, dtype=jnp.int32)
    segment, position = token_layout(seq_lengths, local_index)
    widened = hidden.astype(jnp.float32)
    scale = lax.rsqrt(jnp.mean(widened * widened, axis=1, keepdims=True) + EPSILON)
    normed = (widened * scale * norm_gain[None, :]).astype(jnp.bfloat16)
    query_cols = w_query.shape[1]
    local_heads = query_cols // HEAD
    group_size = QHEADS // KVHEADS
    local_kv = max(local_heads // group_size, 1)
    first_kv = lax.axis_index("tp") * local_heads // group_size
    key_cols = local_kv * HEAD
    key_part = lax.dynamic_slice_in_dim(w_key, first_kv * HEAD, key_cols, 1)
    value_part = lax.dynamic_slice_in_dim(w_value, first_kv * HEAD, key_cols, 1)
    key_bias = lax.dynamic_slice_in_dim(bias_key, first_kv * HEAD, key_cols, 0)
    value_bias = lax.dynamic_slice_in_dim(bias_value, first_kv * HEAD, key_cols, 0)
    pieces = (
        lax.all_gather(w_query, "fsdp", axis=0, tiled=True),
        lax.all_gather(key_part, "fsdp", axis=0, tiled=True),
        lax.all_gather(value_part, "fsdp", axis=0, tiled=True),
    )
    query, keys, values = tuple(
        (jnp.dot(normed, piece, preferred_element_type=jnp.float32) for piece in pieces)
    )
    query = rotary(
        (query + bias_query.astype(jnp.float32)[None, :]).reshape(tok_rows, -1, HEAD), position
    ).astype(jnp.bfloat16)
    keys = rotary(
        (keys + key_bias.astype(jnp.float32)[None, :]).reshape(tok_rows, -1, HEAD), position
    ).astype(jnp.bfloat16)
    values = (values + value_bias.astype(jnp.float32)[None, :]).astype(jnp.bfloat16)
    keys = keys.reshape(tok_rows, key_cols)
    per_kv = local_heads // local_kv
    query_grid = query.reshape(tok_rows, local_kv, per_kv, HEAD)
    start_state = (
        jnp.full((local_kv, per_kv, tok_rows), FLOOR, jnp.float32),
        jnp.zeros((local_kv, per_kv, tok_rows), jnp.float32),
        jnp.zeros((local_kv, per_kv, tok_rows, HEAD), jnp.float32),
    )
    key_piece = lax.all_gather(keys, "fsdp", axis=0, tiled=True)
    value_piece = lax.all_gather(values, "fsdp", axis=0, tiled=True)
    piece_rows = key_piece.shape[0]
    shard_count = max(piece_rows // tok_rows, 1)
    per_block = 1
    for divisor in range(1, 9):
        if shard_count % divisor == 0:
            per_block = divisor
    block_rows = min(per_block * tok_rows, piece_rows)
    block_count = piece_rows // block_rows

    def fold_block(block_number, carried):
        running_max, total, accumulated = carried
        offset = block_number * block_rows
        key_block = lax.dynamic_slice_in_dim(key_piece, offset, block_rows, 0).reshape(
            block_rows, local_kv, HEAD
        )
        value_block = lax.dynamic_slice_in_dim(value_piece, offset, block_rows, 0).reshape(
            block_rows, local_kv, HEAD
        )
        key_index = offset + jnp.arange(block_rows, dtype=jnp.int32)
        key_segment, unused = token_layout(seq_lengths, key_index)
        scores = jnp.einsum(
            "qkgd,nkd->kgqn", query_grid, key_block, preferred_element_type=jnp.float32
        ) * HEAD ** (-0.5)
        allowed = (
            (segment[:, None] == key_segment[None, :])
            & (local_index[:, None] >= key_index[None, :])
        )[None, None]
        scores = jnp.where(allowed, scores, FLOOR)
        new_max = jnp.maximum(running_max, jnp.max(scores, axis=3))
        weights = jnp.where(allowed, jnp.exp(scores - new_max[..., None]), 0.0)
        factor = jnp.exp(running_max - new_max)
        total = total * factor + jnp.sum(weights, axis=3)
        update = jnp.einsum(
            "kgqn,nkd->kgqd",
            weights.astype(jnp.bfloat16),
            value_block,
            preferred_element_type=jnp.float32,
        )
        accumulated = accumulated * factor[..., None] + update
        return (new_max, total, accumulated)

    final_state = lax.fori_loop(0, block_count, fold_block, start_state)
    mixed = final_state[2] / final_state[1][..., None]
    attended = jnp.transpose(mixed, (2, 0, 1, 3)).reshape(tok_rows, query_cols).astype(jnp.bfloat16)
    share_rows = tok_rows // lax.axis_size("tp")
    own_rows = lax.dynamic_slice_in_dim(
        hidden, lax.axis_index("tp") * share_rows, share_rows, 0
    ).astype(jnp.float32)
    terms = jnp.dot(
        attended,
        lax.all_gather(w_out, "fsdp", axis=1, tiled=True),
        preferred_element_type=jnp.float32,
    )
    summed = lax.psum_scatter(
        terms.astype(jnp.bfloat16), "tp", scatter_dimension=0, tiled=True
    ).astype(jnp.float32)
    return own_rows + summed


def solution(mesh):
    in_specs = (
        P("fsdp", None),
        P(),
        P("fsdp", "tp"),
        P("fsdp", None),
        P("fsdp", None),
        P("tp"),
        P(),
        P(),
        P("tp", "fsdp"),
        P(),
    )
    out_specs = P(("fsdp", "tp"), None)
    return jax.shard_map(shards, mesh=mesh, in_specs=in_specs, out_specs=out_specs, check_vma=False)
```

profile of v0, /device:TPU:0, one launch (start us, length us, event | category | flops | bytes accessed | tf_op | source)
XLA Modules:
  0.0 618.8 jit_solution(51648293795599105)
XLA Ops:
  8.4 1.7 constant_dynamic-slice_fusion.2
  13.7 3.1 fusion.15
  16.8 45.9 %all-gather.7.cloned.1.call-done = bf16[8192,256]{1,0:T(8,128)(2,1)} async-done(((bf16[512,256]{1,0:T(8,128)(2,1)}), bf16[8192,256]{1,0:T(8,128)(2,1)}) %all-gather.7.cloned.1.call-update) | async-done | bytes 4194320 | tf_op jit(solution)/shard_map/all_gather | solution.py:59
  62.7 5.6 convolution_add_fusion.2
  69.2 44.6 %all-gather.13.cloned.1.call-done = bf16[8192,256]{1,0:T(8,128)(2,1)} async-done(((bf16[512,256]{1,0:T(8,128)(2,1)}), bf16[8192,256]{1,0:T(8,128)(2,1)}) %all-gather.13.cloned.1.call-update) | async-done | bytes 4194320 | tf_op jit(solution)/shard_map/all_gather | solution.py:60
  113.8 5.4 fusion.20
  120.3 161.7 %all-gather.11.cloned.1.call-done = bf16[8192,2048]{1,0:T(8,128)(2,1)} async-done(((bf16[512,2048]{1,0:T(8,128)(2,1)}), bf16[8192,2048]{1,0:T(8,128)(2,1)}) %all-gather.11.cloned.1.call-update) | async-done | bytes 33554448 | tf_op jit(solution)/shard_map/all_gather | solution.py:58
  282.0 16.5 %convolution_add_fusion = f32[256,2048]{1,0:T(8,128)S(1)} fusion(bf16[8192,2048]{1,0:T(8,128)(2,1)} %all-gather.11.cloned.1.call-done, f32[2048]{0:T(1024)S(1)} %convert_element_type.80, bf16[256,8192]{1,0:T(8,128)(2,1)} %param.12, f32[8192]{0:T(1024)S(1)} %copy-done.8, f32[256]{0:T(256)S(1)} %add_rsqrt_fusion), kind=kOutput, calls=%fused_computation.30 | convolution fusion | flops 8598847488 | bytes 39887872 | tf_op jit(solution)/shard_map/dot_general | solution.py:63
  298.5 1.9 copy.44
  300.3 3.1 slice_negate_fusion
  303.5 3.2 copy.45
  306.6 3.2 copy.46
  313.1 12.0 %all-gather.9.cloned.1.call-done = bf16[4096,256]{0,1:T(8,128)(2,1)} async-done(((bf16[256,256]{0,1:T(8,128)(2,1)}), bf16[4096,256]{0,1:T(8,128)(2,1)}) %all-gather.9.cloned.1.call-update) | async-done | bytes 2097168 | tf_op jit(solution)/shard_map/all_gather | solution.py:80
  325.1 42.6 %all-gather.15.cloned.1.call-done = bf16[4096,256]{1,0:T(8,128)(2,1)} async-done(((bf16[256,256]{1,0:T(8,128)(2,1)}), bf16[4096,256]{1,0:T(8,128)(2,1)}) %all-gather.15.cloned.1.call-update) | async-done | bytes 2097168 | tf_op jit(solution)/shard_map/all_gather | solution.py:81
  367.6 104.9 %while.20 = (s32[]{:T(128)}, f32[2,8,256]{2,1,0:T(8,128)S(1)}, f32[2,8,256]{2,1,0:T(8,128)S(1)}, f32[2,8,256,128]{3,2,1,0:T(8,128)}, s32[256]{0:T(256)S(1)}, /*i...) while((s32[]{:T(128)}, f32[2,8,256]{2,1,0:T(8,128)S(1)}, ...), condition=%wide.region_9.10_spmd.clone, body=%wide.region_5.9_spmd.clone.sunk | while | flops 4407209984 | bytes 125086968 | solution.py:123
  367.6 1.3 constant_dynamic-slice_fusion.6
  369.1 1.4 compare_and_fusion.2
  370.5 15.2 %fusion.45 = (f32[2,8,256]{2,1,0:T(8,128)S(1)}, f32[2,2048,256,8]{2,1,3,0:T(8,128)}) fusion(pred[256,2048]{0,1:T(8,128)(4,1)S(1)} %compare_and_fusion.2, bf16[2048,2,128,1]{0,2,3,1:T(8,128)(2,1)S(1)} %bitcast.72, bf16[256,2,8,128]{3,0,2,1:T(8,128)(2,1)S(1)} %get-tuple-element.451), kind=kOutput, calls=%fused_computation.3.clone.1 | convolution fusion | flops 2172645376 | bytes 36192256 | tf_op jit(solution)/shard_map/while/body/eval_jaxpr/qkgd,nkd->kgqn/dot_general | solution.py:102
  385.7 15.3 %fusion.46 = f32[2,8,256]{2,1,0:T(8,128)S(1)} fusion(f32[2,2048,256,8]{2,1,3,0:T(8,128)} %get-tuple-element.413, f32[2,8,256]{2,1,0:T(8,128)S(1)} %select_maximum_fusion.2, pred[256,2048]{0,1:T(8,128)(4,1)S(1)} %compare_and_fusion.2), kind=kLoop, calls=%fused_computation.5.clone.1 | loop fusion | flops 41938944 | bytes 34111488 | tf_op jit(solution)/shard_map/while/body/eval_jaxpr/reduce_sum | solution.py:113
  401.2 1.4 copy.62
  402.6 17.6 %fusion.48 = f32[2,8,256,128]{3,2,1,0:T(8,128)} fusion(f32[2,8,256,128]{3,2,1,0:T(8,128)} %get-tuple-element.433, bf16[2048,2,128,1]{0,2,3,1:T(8,128)(2,1)} %bitcast.73, f32[2,2048,256,8]{2,1,3,0:T(8,128)} %get-tuple-element.413, f32[2,8,256]{2,1,0:T(8,128)S(1)} %select_maximum_fusion.2, pred[256,2048]{0,1:T(8,128)(4,1)S(1)} %compare_and_fusion.2, ...), kind=kOutput, calls=%fused_computation.9.clone.1 | convolution fusion | flops 2190999552 | bytes 39354368 | tf_op jit(solution)/shard_map/while/body/eval_jaxpr/kgqn,nkd->kgqd/dot_general | solution.py:114
  420.2 1.3 constant_dynamic-slice_fusion.6
  421.7 1.4 compare_and_fusion.2
  423.1 14.1 %fusion.45 = (f32[2,8,256]{2,1,0:T(8,128)S(1)}, f32[2,2048,256,8]{2,1,3,0:T(8,128)}) fusion(pred[256,2048]{0,1:T(8,128)(4,1)S(1)} %compare_and_fusion.2, bf16[2048,2,128,1]{0,2,3,1:T(8,128)(2,1)S(1)} %bitcast.72, bf16[256,2,8,128]{3,0,2,1:T(8,128)(2,1)S(1)} %get-tuple-element.451), kind=kOutput, calls=%fused_computation.3.clone.1 | convolution fusion | flops 2172645376 | bytes 36192256 | tf_op jit(solution)/shard_map/while/body/eval_jaxpr/qkgd,nkd->kgqn/dot_general | solution.py:102
  437.3 15.6 %fusion.46 = f32[2,8,256]{2,1,0:T(8,128)S(1)} fusion(f32[2,2048,256,8]{2,1,3,0:T(8,128)} %get-tuple-element.413, f32[2,8,256]{2,1,0:T(8,128)S(1)} %select_maximum_fusion.2, pred[256,2048]{0,1:T(8,128)(4,1)S(1)} %compare_and_fusion.2), kind=kLoop, calls=%fused_computation.5.clone.1 | loop fusion | flops 41938944 | bytes 34111488 | tf_op jit(solution)/shard_map/while/body/eval_jaxpr/reduce_sum | solution.py:113
  452.9 1.4 copy.62
  454.4 18.2 %fusion.48 = f32[2,8,256,128]{3,2,1,0:T(8,128)} fusion(f32[2,8,256,128]{3,2,1,0:T(8,128)} %get-tuple-element.433, bf16[2048,2,128,1]{0,2,3,1:T(8,128)(2,1)} %bitcast.73, f32[2,2048,256,8]{2,1,3,0:T(8,128)} %get-tuple-element.413, f32[2,8,256]{2,1,0:T(8,128)S(1)} %select_maximum_fusion.2, pred[256,2048]{0,1:T(8,128)(4,1)S(1)} %compare_and_fusion.2, ...), kind=kOutput, calls=%fused_computation.9.clone.1 | convolution fusion | flops 2190999552 | bytes 39354368 | tf_op jit(solution)/shard_map/while/body/eval_jaxpr/kgqn,nkd->kgqd/dot_general | solution.py:114
  472.6 2.1 copy.48
  475.9 59.9 %all-gather.17.cloned.1.call-done = bf16[2048,8192]{1,0:T(8,128)(2,1)} async-done(((bf16[2048,512]{1,0:T(8,128)(2,1)}), bf16[2048,8192]{1,0:T(8,128)(2,1)}) %all-gather.17.cloned.1.call-update) | async-done | bytes 33554448 | tf_op jit(solution)/shard_map/all_gather | solution.py:132
  535.9 16.8 %convolution_convert_fusion = bf16[256,8192]{1,0:T(8,128)(2,1)} fusion(bf16[256,2048]{0,1:T(8,128)(2,1)} %bitcast.77, bf16[2048,8192]{1,0:T(8,128)(2,1)} %all-gather.17.cloned.1.call-done), kind=kOutput, calls=%fused_computation.25 | convolution fusion | flops 8592031744 | bytes 38797312 | tf_op jit(solution)/shard_map/dot_general | solution.py:130
  552.7 54.5 %reduce-scatter.2.cloned.1.call-done = bf16[128,8192]{1,0:T(8,128)(2,1)} async-done(((bf16[256,8192]{1,0:T(8,128)(2,1)}), bf16[128,8192]{1,0:T(8,128)(2,1)}) %reduce-scatter.2.cloned.1.call-update) | async-done | bytes 2097168 | tf_op jit(solution)/shard_map/reduce_scatter | solution.py:135
  607.2 4.8 convert_add_fusion
  (77 shorter events, 12.0 us)
Async XLA Ops:
  6.5 1.0 copy-start
  6.5 7.0 %copy-start.6 = (bf16[512]{0:T(512)(128)(2,1)S(1)}, bf16[512]{0:T(512)(128)(2,1)}, u32[]{:S(2)}) copy-start(bf16[512]{0:T(512)(128)(2,1)} %param.18) | copy-start | bytes 3076
  6.5 56.1 %all-gather.7.cloned.1.call-start = ((), (), s32[]{:S(2)}) async-start(), calls=%async_computation.1 | async-start | bytes 4456448 | tf_op jit(solution)/shard_map/all_gather | solution.py:59
  8.3 54.4 %copy-start.8 = (f32[8192]{0:T(1024)S(1)}, f32[8192]{0:T(1024)}, u32[]{:S(2)}) copy-start(f32[8192]{0:T(1024)} %param.13) | copy-start | bytes 98308
  8.3 105.4 %all-gather.13.cloned.1.call-start = ((), (), s32[]{:S(2)}) async-start(), calls=%async_computation.4 | async-start | bytes 4456448 | tf_op jit(solution)/shard_map/all_gather | solution.py:60
  10.1 271.9 %all-gather.11.cloned.1.call-start = ((), (), s32[]{:S(2)}) async-start(), calls=%async_computation.3 | async-start | bytes 35651584 | tf_op jit(solution)/shard_map/all_gather | solution.py:58
  10.9 314.2 %all-gather.9.cloned.1.call-start = ((), (), s32[]{:S(2)}) async-start(), calls=%async_computation.2 | async-start | bytes 2228224 | tf_op jit(solution)/shard_map/all_gather | solution.py:80
  16.8 52.3 %copy-start.7 = (bf16[512]{0:T(512)(128)(2,1)S(1)}, bf16[512]{0:T(512)(128)(2,1)}, u32[]{:S(2)}) copy-start(bf16[512]{0:T(512)(128)(2,1)} %param.19) | copy-start | bytes 3076
  69.0 298.6 %all-gather.15.cloned.1.call-start = ((), (), s32[]{:S(2)}) async-start(), calls=%async_computation.5 | async-start | bytes 2228224 | tf_op jit(solution)/shard_map/all_gather | solution.py:81
  69.2 50.9 %copy-start.5 = (bf16[2048]{0:T(1024)(128)(2,1)S(1)}, bf16[2048]{0:T(1024)(128)(2,1)}, u32[]{:S(2)}) copy-start(bf16[2048]{0:T(1024)(128)(2,1)} %param.17) | copy-start | bytes 12292
  69.2 50.9 %copy-start.9 = (s32[4]{0:T(128)S(1)}, s32[4]{0:T(128)}, u32[]{:S(2)}) copy-start(s32[4]{0:T(128)} %param.21) | copy-start | bytes 52
  119.2 416.6 %all-gather.17.cloned.1.call-start = ((), (), s32[]{:S(2)}) async-start(), calls=%async_computation.6 | async-start | bytes 35651584 | tf_op jit(solution)/shard_map/all_gather | solution.py:132
  119.8 487.3 %reduce-scatter.2.cloned.1.call-start = ((), (), s32[]{:S(2)}) async-start(), calls=%async_computation.7 | async-start | bytes 6291456 | tf_op jit(solution)/shard_map/reduce_scatter | solution.py:135
  309.9 1.6 copy-start.3
  309.9 2.2 copy-start.4
  385.7 15.3 %copy-start.2 = (bf16[4096,256]{1,0:T(8,128)(2,1)S(1)}, bf16[4096,256]{1,0:T(8,128)(2,1)}, u32[]{:S(2)}) copy-start(bf16[4096,256]{1,0:T(8,128)(2,1)} %get-tuple-element.452) | copy-start | bytes 6291460 | tf_op jit(solution)/shard_map/while
  437.3 15.6 %copy-start.2 = (bf16[4096,256]{1,0:T(8,128)(2,1)S(1)}, bf16[4096,256]{1,0:T(8,128)(2,1)}, u32[]{:S(2)}) copy-start(bf16[4096,256]{1,0:T(8,128)(2,1)} %get-tuple-element.452) | copy-start | bytes 6291460 | tf_op jit(solution)/shard_map/while
  552.6 59.3 %copy-start.1 = (bf16[512,512]{1,0:T(8,128)(2,1)S(1)}, bf16[512,512]{1,0:T(8,128)(2,1)}, u32[]{:S(2)}) copy-start(bf16[512,512]{1,0:T(8,128)(2,1)} %param.15) | copy-start | bytes 1572868
Sparse Core Ops, SparseCore 0:
  9.5 53.1 all-gather.6
  64.8 48.8 all-gather.12
  115.4 166.5 all-gather.10
  284.0 41.0 all-gather.8
  327.1 40.5 all-gather.14
  369.1 166.7 all-gather.16
  552.8 54.3 reduce-scatter.1
where the time goes:
time: 619 us
  waiting for transfers between devices  423 us (68%)
  matrix products  109 us (18%)
  other arithmetic  50.7 us (8%)
  local copies, waits for them, and re-layouts  21.9 us (4%)
  between operations  13.7 us (2%)
    all_gather x1, waiting for transfers between devices, shards(): lax.all_gather(w_query, 'fsdp', axis=0, tiled=True)  162 us
    all_gather x1, waiting for transfers between devices, shards(): lax.all_gather(w_out, 'fsdp', axis=1, tiled=True)  59.9 us
    reduce_scatter x1, waiting for transfers between devices, shards(): lax.psum_scatter(terms.astype(jnp.bfloat16), 'tp', scatter_dimension=0, t...  54.5 us
    all_gather x1, waiting for transfers between devices, shards(): lax.all_gather(key_part, 'fsdp', axis=0, tiled=True)  45.9 us
    all_gather x1, waiting for transfers between devices, shards(): lax.all_gather(value_part, 'fsdp', axis=0, tiled=True)  44.6 us
    all_gather x1, waiting for transfers between devices, shards(): value_piece = lax.all_gather(values, 'fsdp', axis=0, tiled=True)  42.6 us
    dot_general x2, matrix products, fold_block(): jnp.einsum('kgqn,nkd->kgqd', weights.astype(jnp.bfloat16), value_block, p...  35.9 us
    reduce_sum x2, other arithmetic, fold_block(): total = total * factor + jnp.sum(weights, axis=3)  30.9 us
  transfers between devices with their start and end apart: 7, of which 7 were waited for; matrix products, arithmetic and copies ran while one was open for 25% of the time, Pallas kernels for 0%

commit v1 on v0

--- a/solution.py
+++ b/solution.py
@@ -78,7 +78,16 @@
         jnp.zeros((local_kv, per_kv, tok_rows, HEAD), jnp.float32),
     )
     key_piece = lax.all_gather(keys, "fsdp", axis=0, tiled=True)
-    value_piece = lax.all_gather(values, "fsdp", axis=0, tiled=True)
+    n_lanes = lax.axis_size("fsdp")
+    res = sorted(((k0, (k0 + 1) % n_lanes) for k0 in range(n_lanes)))
+    frame_out = values
+    copies = [frame_out]
+    for dev_i in range(1, n_lanes):
+        frame_out = lax.ppermute(frame_out, axis_name="fsdp", perm=res)
+        copies.insert(0, frame_out)
+    row_out = jnp.concatenate(copies, 0)
+    o_now = lax.axis_index("fsdp") + 1
+    value_piece = jnp.roll(row_out, o_now * values.shape[0], 0)
     piece_rows = key_piece.shape[0]
     shard_count = max(piece_rows // tok_rows, 1)
     per_block = 1

time: 619 us -> 597 us (0.964)
  waiting for transfers between devices: 423 us -> 399 us
    ppermute x0 -> x15, waiting for transfers between devices: none -> 148 us  [shards(): frame_out = lax.ppermute(frame_out, axis_name='fsdp', perm=res)]
    all_gather x1, waiting for transfers between devices: 162 us -> 33.6 us  [shards(): lax.all_gather(w_query, 'fsdp', axis=0, tiled=True)]
    all_gather x1 -> x0, waiting for transfers between devices: 42.6 us -> none  [shards(): value_piece = lax.all_gather(values, 'fsdp', axis=0, tiled=True)]
  transfers between devices with their start and end apart: 7 -> 21, of which waited for: 7 -> 21; matrix products, arithmetic and copies ran while one was open for 25% -> 26% of each run, Pallas kernels for 0% -> 0%
where the time goes in v1:
time: 597 us; the launch traced here: 596 us
  waiting for transfers between devices  399 us (67%)
  matrix products  109 us (18%)
  other arithmetic  50.5 us (8%)
  local copies, waits for them, and re-layouts  23.5 us (4%)
  between operations  13.9 us (2%)
    ppermute x15, waiting for transfers between devices, shards(): frame_out = lax.ppermute(frame_out, axis_name='fsdp', perm=res)  148 us
    all_gather x1, waiting for transfers between devices, shards(): lax.all_gather(w_out, 'fsdp', axis=1, tiled=True)  60.7 us
    reduce_scatter x1, waiting for transfers between devices, shards(): lax.psum_scatter(terms.astype(jnp.bfloat16), 'tp', scatter_dimension=0, t...  54.5 us
    all_gather x1, waiting for transfers between devices, shards(): lax.all_gather(key_part, 'fsdp', axis=0, tiled=True)  45.9 us
    all_gather x1, waiting for transfers between devices, shards(): lax.all_gather(value_part, 'fsdp', axis=0, tiled=True)  44 us
    dot_general x2, matrix products, fold_block(): jnp.einsum('kgqn,nkd->kgqd', weights.astype(jnp.bfloat16), value_block, p...  35.8 us
    all_gather x1, waiting for transfers between devices, shards(): lax.all_gather(w_query, 'fsdp', axis=0, tiled=True)  33.6 us
    reduce_sum x2, other arithmetic, fold_block(): total = total * factor + jnp.sum(weights, axis=3)  30.6 us
  transfers between devices with their start and end apart: 21, of which 21 were waited for; matrix products, arithmetic and copies ran while one was open for 26% of the time, Pallas kernels for 0%

profile of v1, /device:TPU:0, one launch (start us, length us, event | category | flops | bytes accessed | tf_op | source)
XLA Modules:
  0.0 596.3 jit_solution(7130515803802161593)
XLA Ops:
  16.7 45.9 %all-gather.6.cloned.1.call-done = bf16[8192,256]{1,0:T(8,128)(2,1)} async-done(((bf16[512,256]{1,0:T(8,128)(2,1)}), bf16[8192,256]{1,0:T(8,128)(2,1)}) %all-gather.6.cloned.1.call-update) | async-done | bytes 4194320 | tf_op jit(solution)/shard_map/all_gather | solution.py:59
  62.6 5.6 convolution_add_fusion.2
  69.7 44.0 %all-gather.12.cloned.1.call-done = bf16[8192,256]{1,0:T(8,128)(2,1)} async-done(((bf16[512,256]{1,0:T(8,128)(2,1)}), bf16[8192,256]{1,0:T(8,128)(2,1)}) %all-gather.12.cloned.1.call-update) | async-done | bytes 4194320 | tf_op jit(solution)/shard_map/all_gather | solution.py:60
  113.7 4.8 fusion.20
  118.8 7.7 %collective-permute-done = bf16[256,256]{1,0:T(8,128)(2,1)S(1)} collective-permute-done((bf16[256,256]{1,0:T(8,128)(2,1)S(1)}, bf16[256,256]{1,0:T(8,128)(2,1)S(1)}, u32[]{:S(2)}, u32[]{:S(2)}) %collective-permute-start) | collective-permute-done | bytes 131104 | tf_op jit(solution)/shard_map/ppermute | solution.py:86
  126.5 10.0 %collective-permute-done.1 = bf16[256,256]{1,0:T(8,128)(2,1)S(1)} collective-permute-done((bf16[256,256]{1,0:T(8,128)(2,1)S(1)}, bf16[256,256]{1,0:T(8,128)(2,1)S(1)}, u32[]{:S(2)}, u32[]{:S(2)}) %collective-permute-start.1) | collective-permute-done | bytes 131104 | tf_op jit(solution)/shard_map/ppermute | solution.py:86
  136.5 10.0 %collective-permute-done.2 = bf16[256,256]{1,0:T(8,128)(2,1)S(1)} collective-permute-done((bf16[256,256]{1,0:T(8,128)(2,1)S(1)}, bf16[256,256]{1,0:T(8,128)(2,1)S(1)}, u32[]{:S(2)}, u32[]{:S(2)}) %collective-permute-start.2) | collective-permute-done | bytes 131104 | tf_op jit(solution)/shard_map/ppermute | solution.py:86
  146.6 10.0 %collective-permute-done.3 = bf16[256,256]{1,0:T(8,128)(2,1)S(1)} collective-permute-done((bf16[256,256]{1,0:T(8,128)(2,1)S(1)}, bf16[256,256]{1,0:T(8,128)(2,1)S(1)}, u32[]{:S(2)}, u32[]{:S(2)}) %collective-permute-start.3) | collective-permute-done | bytes 131104 | tf_op jit(solution)/shard_map/ppermute | solution.py:86
  156.6 10.0 %collective-permute-done.4 = bf16[256,256]{1,0:T(8,128)(2,1)S(1)} collective-permute-done((bf16[256,256]{1,0:T(8,128)(2,1)S(1)}, bf16[256,256]{1,0:T(8,128)(2,1)S(1)}, u32[]{:S(2)}, u32[]{:S(2)}) %collective-permute-start.4) | collective-permute-done | bytes 131104 | tf_op jit(solution)/shard_map/ppermute | solution.py:86
  166.6 10.0 %collective-permute-done.5 = bf16[256,256]{1,0:T(8,128)(2,1)S(1)} collective-permute-done((bf16[256,256]{1,0:T(8,128)(2,1)S(1)}, bf16[256,256]{1,0:T(8,128)(2,1)S(1)}, u32[]{:S(2)}, u32[]{:S(2)}) %collective-permute-start.5) | collective-permute-done | bytes 131104 | tf_op jit(solution)/shard_map/ppermute | solution.py:86
  176.6 10.0 %collective-permute-done.6 = bf16[256,256]{1,0:T(8,128)(2,1)S(1)} collective-permute-done((bf16[256,256]{1,0:T(8,128)(2,1)S(1)}, bf16[256,256]{1,0:T(8,128)(2,1)S(1)}, u32[]{:S(2)}, u32[]{:S(2)}) %collective-permute-start.6) | collective-permute-done | bytes 131104 | tf_op jit(solution)/shard_map/ppermute | solution.py:86
  186.7 10.0 %collective-permute-done.7 = bf16[256,256]{1,0:T(8,128)(2,1)S(1)} collective-permute-done((bf16[256,256]{1,0:T(8,128)(2,1)S(1)}, bf16[256,256]{1,0:T(8,128)(2,1)S(1)}, u32[]{:S(2)}, u32[]{:S(2)}) %collective-permute-start.7) | collective-permute-done | bytes 131104 | tf_op jit(solution)/shard_map/ppermute | solution.py:86
  196.7 10.0 %collective-permute-done.8 = bf16[256,256]{1,0:T(8,128)(2,1)S(1)} collective-permute-done((bf16[256,256]{1,0:T(8,128)(2,1)S(1)}, bf16[256,256]{1,0:T(8,128)(2,1)S(1)}, u32[]{:S(2)}, u32[]{:S(2)}) %collective-permute-start.8) | collective-permute-done | bytes 131104 | tf_op jit(solution)/shard_map/ppermute | solution.py:86
  206.7 10.0 %collective-permute-done.9 = bf16[256,256]{1,0:T(8,128)(2,1)S(1)} collective-permute-done((bf16[256,256]{1,0:T(8,128)(2,1)S(1)}, bf16[256,256]{1,0:T(8,128)(2,1)S(1)}, u32[]{:S(2)}, u32[]{:S(2)}) %collective-permute-start.9) | collective-permute-done | bytes 131104 | tf_op jit(solution)/shard_map/ppermute | solution.py:86
  216.8 10.0 %collective-permute-done.10 = bf16[256,256]{1,0:T(8,128)(2,1)S(1)} collective-permute-done((bf16[256,256]{1,0:T(8,128)(2,1)S(1)}, bf16[256,256]{1,0:T(8,128)(2,1)S(1)}, u32[]{:S(2)}, u32[]{:S(2)}) %collective-permute-start.10) | collective-permute-done | bytes 131104 | tf_op jit(solution)/shard_map/ppermute | solution.py:86
  226.8 10.0 %collective-permute-done.11 = bf16[256,256]{1,0:T(8,128)(2,1)S(1)} collective-permute-done((bf16[256,256]{1,0:T(8,128)(2,1)S(1)}, bf16[256,256]{1,0:T(8,128)(2,1)S(1)}, u32[]{:S(2)}, u32[]{:S(2)}) %collective-permute-start.11) | collective-permute-done | bytes 131104 | tf_op jit(solution)/shard_map/ppermute | solution.py:86
  236.8 10.0 %collective-permute-done.12 = bf16[256,256]{1,0:T(8,128)(2,1)S(1)} collective-permute-done((bf16[256,256]{1,0:T(8,128)(2,1)S(1)}, bf16[256,256]{1,0:T(8,128)(2,1)S(1)}, u32[]{:S(2)}, u32[]{:S(2)}) %collective-permute-start.12) | collective-permute-done | bytes 131104 | tf_op jit(solution)/shard_map/ppermute | solution.py:86
  246.8 10.0 %collective-permute-done.13 = bf16[256,256]{1,0:T(8,128)(2,1)S(1)} collective-permute-done((bf16[256,256]{1,0:T(8,128)(2,1)S(1)}, bf16[256,256]{1,0:T(8,128)(2,1)S(1)}, u32[]{:S(2)}, u32[]{:S(2)}) %collective-permute-start.13) | collective-permute-done | bytes 131104 | tf_op jit(solution)/shard_map/ppermute | solution.py:86
  257.1 9.8 %collective-permute-done.14 = bf16[256,256]{1,0:T(8,128)(2,1)S(1)} collective-permute-done((bf16[256,256]{1,0:T(8,128)(2,1)S(1)}, bf16[256,256]{1,0:T(8,128)(2,1)S(1)}, u32[]{:S(2)}, u32[]{:S(2)}) %collective-permute-start.14) | collective-permute-done | bytes 131104 | tf_op jit(solution)/shard_map/ppermute | solution.py:86
  269.0 33.6 %all-gather.10.cloned.1.call-done = bf16[8192,2048]{1,0:T(8,128)(2,1)} async-done(((bf16[512,2048]{1,0:T(8,128)(2,1)}), bf16[8192,2048]{1,0:T(8,128)(2,1)}) %all-gather.10.cloned.1.call-update) | async-done | bytes 33554448 | tf_op jit(solution)/shard_map/all_gather | solution.py:58
  302.6 16.5 %convolution_add_fusion = f32[256,2048]{1,0:T(8,128)S(1)} fusion(bf16[8192,2048]{1,0:T(8,128)(2,1)} %all-gather.10.cloned.1.call-done, f32[2048]{0:T(1024)S(1)} %convert_element_type.80, bf16[256,8192]{1,0:T(8,128)(2,1)} %param.12, f32[8192]{0:T(1024)S(1)} %copy-done.8, f32[256]{0:T(256)S(1)} %add_rsqrt_fusion), kind=kOutput, calls=%fused_computation.30 | convolution fusion | flops 8598847488 | bytes 39887872 | tf_op jit(solution)/shard_map/dot_general | solution.py:63
  333.6 11.2 %all-gather.8.cloned.1.call-done = bf16[4096,256]{0,1:T(8,128)(2,1)} async-done(((bf16[256,256]{0,1:T(8,128)(2,1)}), bf16[4096,256]{0,1:T(8,128)(2,1)}) %all-gather.8.cloned.1.call-update) | async-done | bytes 2097168 | tf_op jit(solution)/shard_map/all_gather | solution.py:80
  344.8 104.7 %while.20 = (s32[]{:T(128)}, f32[2,8,256]{2,1,0:T(8,128)S(1)}, f32[2,8,256]{2,1,0:T(8,128)S(1)}, f32[2,8,256,128]{3,2,1,0:T(8,128)}, s32[256]{0:T(256)S(1)}, /*i...) while((s32[]{:T(128)}, f32[2,8,256]{2,1,0:T(8,128)S(1)}, ...), condition=%wide.region_9.10_spmd.clone, body=%wide.region_5.9_spmd.clone.sunk | while | flops 4407209984 | bytes 125086968 | solution.py:132
  347.7 15.2 %fusion.45 = (f32[2,8,256]{2,1,0:T(8,128)S(1)}, f32[2,2048,256,8]{2,1,3,0:T(8,128)}) fusion(pred[256,2048]{0,1:T(8,128)(4,1)S(1)} %compare_and_fusion.2, bf16[2048,2,128,1]{0,2,3,1:T(8,128)(2,1)S(1)} %bitcast.72, bf16[256,2,8,128]{3,0,2,1:T(8,128)(2,1)S(1)} %get-tuple-element.451), kind=kOutput, calls=%fused_computation.3.clone.1 | convolution fusion | flops 2172645376 | bytes 36192256 | tf_op jit(solution)/shard_map/while/body/eval_jaxpr/qkgd,nkd->kgqn/dot_general | solution.py:111
  362.9 15.3 %fusion.46 = f32[2,8,256]{2,1,0:T(8,128)S(1)} fusion(f32[2,2048,256,8]{2,1,3,0:T(8,128)} %get-tuple-element.413, f32[2,8,256]{2,1,0:T(8,128)S(1)} %select_maximum_fusion.2, pred[256,2048]{0,1:T(8,128)(4,1)S(1)} %compare_and_fusion.2), kind=kLoop, calls=%fused_computation.5.clone.1 | loop fusion | flops 41938944 | bytes 34111488 | tf_op jit(solution)/shard_map/while/body/eval_jaxpr/reduce_sum | solution.py:122
  379.7 17.6 %fusion.48 = f32[2,8,256,128]{3,2,1,0:T(8,128)} fusion(f32[2,8,256,128]{3,2,1,0:T(8,128)} %get-tuple-element.433, bf16[2048,2,128,1]{0,2,3,1:T(8,128)(2,1)} %bitcast.73, f32[2,2048,256,8]{2,1,3,0:T(8,128)} %get-tuple-element.413, f32[2,8,256]{2,1,0:T(8,128)S(1)} %select_maximum_fusion.2, pred[256,2048]{0,1:T(8,128)(4,1)S(1)} %compare_and_fusion.2, ...), kind=kOutput, calls=%fused_computation.9.clone.1 | convolution fusion | flops 2190999552 | bytes 39354368 | tf_op jit(solution)/shard_map/while/body/eval_jaxpr/kgqn,nkd->kgqd/dot_general | solution.py:123
  400.2 14.1 %fusion.45 = (f32[2,8,256]{2,1,0:T(8,128)S(1)}, f32[2,2048,256,8]{2,1,3,0:T(8,128)}) fusion(pred[256,2048]{0,1:T(8,128)(4,1)S(1)} %compare_and_fusion.2, bf16[2048,2,128,1]{0,2,3,1:T(8,128)(2,1)S(1)} %bitcast.72, bf16[256,2,8,128]{3,0,2,1:T(8,128)(2,1)S(1)} %get-tuple-element.451), kind=kOutput, calls=%fused_computation.3.clone.1 | convolution fusion | flops 2172645376 | bytes 36192256 | tf_op jit(solution)/shard_map/while/body/eval_jaxpr/qkgd,nkd->kgqn/dot_general | solution.py:111
  414.4 15.3 %fusion.46 = f32[2,8,256]{2,1,0:T(8,128)S(1)} fusion(f32[2,2048,256,8]{2,1,3,0:T(8,128)} %get-tuple-element.413, f32[2,8,256]{2,1,0:T(8,128)S(1)} %select_maximum_fusion.2, pred[256,2048]{0,1:T(8,128)(4,1)S(1)} %compare_and_fusion.2), kind=kLoop, calls=%fused_computation.5.clone.1 | loop fusion | flops 41938944 | bytes 34111488 | tf_op jit(solution)/shard_map/while/body/eval_jaxpr/reduce_sum | solution.py:122
  431.3 18.2 %fusion.48 = f32[2,8,256,128]{3,2,1,0:T(8,128)} fusion(f32[2,8,256,128]{3,2,1,0:T(8,128)} %get-tuple-element.433, bf16[2048,2,128,1]{0,2,3,1:T(8,128)(2,1)} %bitcast.73, f32[2,2048,256,8]{2,1,3,0:T(8,128)} %get-tuple-element.413, f32[2,8,256]{2,1,0:T(8,128)S(1)} %select_maximum_fusion.2, pred[256,2048]{0,1:T(8,128)(4,1)S(1)} %compare_and_fusion.2, ...), kind=kOutput, calls=%fused_computation.9.clone.1 | convolution fusion | flops 2190999552 | bytes 39354368 | tf_op jit(solution)/shard_map/while/body/eval_jaxpr/kgqn,nkd->kgqd/dot_general | solution.py:123
  452.6 60.7 %all-gather.14.cloned.1.call-done = bf16[2048,8192]{1,0:T(8,128)(2,1)} async-done(((bf16[2048,512]{1,0:T(8,128)(2,1)}), bf16[2048,8192]{1,0:T(8,128)(2,1)}) %all-gather.14.cloned.1.call-update) | async-done | bytes 33554448 | tf_op jit(solution)/shard_map/all_gather | solution.py:141
  513.3 16.8 %convolution_convert_fusion = bf16[256,8192]{1,0:T(8,128)(2,1)} fusion(bf16[256,2048]{0,1:T(8,128)(2,1)} %bitcast.77, bf16[2048,8192]{1,0:T(8,128)(2,1)} %all-gather.14.cloned.1.call-done), kind=kOutput, calls=%fused_computation.25 | convolution fusion | flops 8592031744 | bytes 38797312 | tf_op jit(solution)/shard_map/dot_general | solution.py:139
  530.1 54.5 %reduce-scatter.2.cloned.1.call-done = bf16[128,8192]{1,0:T(8,128)(2,1)} async-done(((bf16[256,8192]{1,0:T(8,128)(2,1)}), bf16[128,8192]{1,0:T(8,128)(2,1)}) %reduce-scatter.2.cloned.1.call-update) | async-done | bytes 2097168 | tf_op jit(solution)/shard_map/reduce_scatter | solution.py:144
  (137 shorter events, 45.1 us)
Async XLA Ops:
  6.5 1.0 copy-start
  6.5 7.0 %copy-start.6 = (bf16[512]{0:T(512)(128)(2,1)S(1)}, bf16[512]{0:T(512)(128)(2,1)}, u32[]{:S(2)}) copy-start(bf16[512]{0:T(512)(128)(2,1)} %param.18) | copy-start | bytes 3076
  6.5 56.1 %all-gather.6.cloned.1.call-start = ((), (), s32[]{:S(2)}) async-start(), calls=%async_computation.1 | async-start | bytes 4456448 | tf_op jit(solution)/shard_map/all_gather | solution.py:59
  8.3 54.3 %copy-start.8 = (f32[8192]{0:T(1024)S(1)}, f32[8192]{0:T(1024)}, u32[]{:S(2)}) copy-start(f32[8192]{0:T(1024)} %param.13) | copy-start | bytes 98308
  8.3 105.4 %all-gather.12.cloned.1.call-start = ((), (), s32[]{:S(2)}) async-start(), calls=%async_computation.4 | async-start | bytes 4456448 | tf_op jit(solution)/shard_map/all_gather | solution.py:60
  10.1 292.5 %all-gather.10.cloned.1.call-start = ((), (), s32[]{:S(2)}) async-start(), calls=%async_computation.3 | async-start | bytes 35651584 | tf_op jit(solution)/shard_map/all_gather | solution.py:58
  10.8 334.0 %all-gather.8.cloned.1.call-start = ((), (), s32[]{:S(2)}) async-start(), calls=%async_computation.2 | async-start | bytes 2228224 | tf_op jit(solution)/shard_map/all_gather | solution.py:80
  68.2 1.4 copy-start.7
  69.0 444.3 %all-gather.14.cloned.1.call-start = ((), (), s32[]{:S(2)}) async-start(), calls=%async_computation.5 | async-start | bytes 35651584 | tf_op jit(solution)/shard_map/all_gather | solution.py:141
  69.6 515.1 %reduce-scatter.2.cloned.1.call-start = ((), (), s32[]{:S(2)}) async-start(), calls=%async_computation.6 | async-start | bytes 6291456 | tf_op jit(solution)/shard_map/reduce_scatter | solution.py:144
  69.7 187.1 %copy-start.5 = (bf16[2048]{0:T(1024)(128)(2,1)S(1)}, bf16[2048]{0:T(1024)(128)(2,1)}, u32[]{:S(2)}) copy-start(bf16[2048]{0:T(1024)(128)(2,1)} %param.17) | copy-start | bytes 12292
  69.7 187.2 %copy-start.9 = (s32[4]{0:T(128)S(1)}, s32[4]{0:T(128)}, u32[]{:S(2)}) copy-start(s32[4]{0:T(128)} %param.21) | copy-start | bytes 52
  118.5 8.0 %collective-permute-start = (bf16[256,256]{1,0:T(8,128)(2,1)S(1)}, bf16[256,256]{1,0:T(8,128)(2,1)S(1)}, u32[]{:S(2)}, u32[]{:S(2)}) collective-permute-start(bf16[256,256]{1,0:T(8,128)(2,1)S(1)} %fusion.20), channel_id=1, source_target_pairs={{0,2},{2,4},{4,6},{6,8},{8,10},{10,12},{12,14},{14,16},{16,18},{18... | collective-permute-start | bytes 393224 | tf_op jit(solution)/shard_map/ppermute | solution.py:86
  126.5 10.0 %collective-permute-start.1 = (bf16[256,256]{1,0:T(8,128)(2,1)S(1)}, bf16[256,256]{1,0:T(8,128)(2,1)S(1)}, u32[]{:S(2)}, u32[]{:S(2)}) collective-permute-start(bf16[256,256]{1,0:T(8,128)(2,1)S(1)} %collective-permute-done), channel_id=1, source_target_pairs={{0,2},{2,4},{4,6},{6,8},{8,10},{10,12},{12,14},{14,16},{16,18},{18... | collective-permute-start | bytes 393224 | tf_op jit(solution)/shard_map/ppermute | solution.py:86
  136.5 10.0 %collective-permute-start.2 = (bf16[256,256]{1,0:T(8,128)(2,1)S(1)}, bf16[256,256]{1,0:T(8,128)(2,1)S(1)}, u32[]{:S(2)}, u32[]{:S(2)}) collective-permute-start(bf16[256,256]{1,0:T(8,128)(2,1)S(1)} %collective-permute-done.1), channel_id=1, source_target_pairs={{0,2},{2,4},{4,6},{6,8},{8,10},{10,12},{12,14},{14,16},{16,18},{18... | collective-permute-start | bytes 393224 | tf_op jit(solution)/shard_map/ppermute | solution.py:86
  146.5 10.0 %collective-permute-start.3 = (bf16[256,256]{1,0:T(8,128)(2,1)S(1)}, bf16[256,256]{1,0:T(8,128)(2,1)S(1)}, u32[]{:S(2)}, u32[]{:S(2)}) collective-permute-start(bf16[256,256]{1,0:T(8,128)(2,1)S(1)} %collective-permute-done.2), channel_id=1, source_target_pairs={{0,2},{2,4},{4,6},{6,8},{8,10},{10,12},{12,14},{14,16},{16,18},{18... | collective-permute-start | bytes 393224 | tf_op jit(solution)/shard_map/ppermute | solution.py:86
  156.6 10.0 %collective-permute-start.4 = (bf16[256,256]{1,0:T(8,128)(2,1)S(1)}, bf16[256,256]{1,0:T(8,128)(2,1)S(1)}, u32[]{:S(2)}, u32[]{:S(2)}) collective-permute-start(bf16[256,256]{1,0:T(8,128)(2,1)S(1)} %collective-permute-done.3), channel_id=1, source_target_pairs={{0,2},{2,4},{4,6},{6,8},{8,10},{10,12},{12,14},{14,16},{16,18},{18... | collective-permute-start | bytes 393224 | tf_op jit(solution)/shard_map/ppermute | solution.py:86
  166.6 10.0 %collective-permute-start.5 = (bf16[256,256]{1,0:T(8,128)(2,1)S(1)}, bf16[256,256]{1,0:T(8,128)(2,1)S(1)}, u32[]{:S(2)}, u32[]{:S(2)}) collective-permute-start(bf16[256,256]{1,0:T(8,128)(2,1)S(1)} %collective-permute-done.4), channel_id=1, source_target_pairs={{0,2},{2,4},{4,6},{6,8},{8,10},{10,12},{12,14},{14,16},{16,18},{18... | collective-permute-start | bytes 393224 | tf_op jit(solution)/shard_map/ppermute | solution.py:86
  176.6 10.0 %collective-permute-start.6 = (bf16[256,256]{1,0:T(8,128)(2,1)S(1)}, bf16[256,256]{1,0:T(8,128)(2,1)S(1)}, u32[]{:S(2)}, u32[]{:S(2)}) collective-permute-start(bf16[256,256]{1,0:T(8,128)(2,1)S(1)} %collective-permute-done.5), channel_id=1, source_target_pairs={{0,2},{2,4},{4,6},{6,8},{8,10},{10,12},{12,14},{14,16},{16,18},{18... | collective-permute-start | bytes 393224 | tf_op jit(solution)/shard_map/ppermute | solution.py:86
  186.7 10.0 %collective-permute-start.7 = (bf16[256,256]{1,0:T(8,128)(2,1)S(1)}, bf16[256,256]{1,0:T(8,128)(2,1)S(1)}, u32[]{:S(2)}, u32[]{:S(2)}) collective-permute-start(bf16[256,256]{1,0:T(8,128)(2,1)S(1)} %collective-permute-done.6), channel_id=1, source_target_pairs={{0,2},{2,4},{4,6},{6,8},{8,10},{10,12},{12,14},{14,16},{16,18},{18... | collective-permute-start | bytes 393224 | tf_op jit(solution)/shard_map/ppermute | solution.py:86
  196.7 10.0 %collective-permute-start.8 = (bf16[256,256]{1,0:T(8,128)(2,1)S(1)}, bf16[256,256]{1,0:T(8,128)(2,1)S(1)}, u32[]{:S(2)}, u32[]{:S(2)}) collective-permute-start(bf16[256,256]{1,0:T(8,128)(2,1)S(1)} %collective-permute-done.7), channel_id=1, source_target_pairs={{0,2},{2,4},{4,6},{6,8},{8,10},{10,12},{12,14},{14,16},{16,18},{18... | collective-permute-start | bytes 393224 | tf_op jit(solution)/shard_map/ppermute | solution.py:86
  206.7 10.0 %collective-permute-start.9 = (bf16[256,256]{1,0:T(8,128)(2,1)S(1)}, bf16[256,256]{1,0:T(8,128)(2,1)S(1)}, u32[]{:S(2)}, u32[]{:S(2)}) collective-permute-start(bf16[256,256]{1,0:T(8,128)(2,1)S(1)} %collective-permute-done.8), channel_id=1, source_target_pairs={{0,2},{2,4},{4,6},{6,8},{8,10},{10,12},{12,14},{14,16},{16,18},{18... | collective-permute-start | bytes 393224 | tf_op jit(solution)/shard_map/ppermute | solution.py:86
  216.7 10.0 %collective-permute-start.10 = (bf16[256,256]{1,0:T(8,128)(2,1)S(1)}, bf16[256,256]{1,0:T(8,128)(2,1)S(1)}, u32[]{:S(2)}, u32[]{:S(2)}) collective-permute-start(bf16[256,256]{1,0:T(8,128)(2,1)S(1)} %collective-permute-done.9), channel_id=1, source_target_pairs={{0,2},{2,4},{4,6},{6,8},{8,10},{10,12},{12,14},{14,16},{16,18},{18... | collective-permute-start | bytes 393224 | tf_op jit(solution)/shard_map/ppermute | solution.py:86
  226.8 10.0 %collective-permute-start.11 = (bf16[256,256]{1,0:T(8,128)(2,1)S(1)}, bf16[256,256]{1,0:T(8,128)(2,1)S(1)}, u32[]{:S(2)}, u32[]{:S(2)}) collective-permute-start(bf16[256,256]{1,0:T(8,128)(2,1)S(1)} %collective-permute-done.10), channel_id=1, source_target_pairs={{0,2},{2,4},{4,6},{6,8},{8,10},{10,12},{12,14},{14,16},{16,18},{18... | collective-permute-start | bytes 393224 | tf_op jit(solution)/shard_map/ppermute | solution.py:86
  236.8 10.0 %collective-permute-start.12 = (bf16[256,256]{1,0:T(8,128)(2,1)S(1)}, bf16[256,256]{1,0:T(8,128)(2,1)S(1)}, u32[]{:S(2)}, u32[]{:S(2)}) collective-permute-start(bf16[256,256]{1,0:T(8,128)(2,1)S(1)} %collective-permute-done.11), channel_id=1, source_target_pairs={{0,2},{2,4},{4,6},{6,8},{8,10},{10,12},{12,14},{14,16},{16,18},{18... | collective-permute-start | bytes 393224 | tf_op jit(solution)/shard_map/ppermute | solution.py:86
  246.8 10.0 %collective-permute-start.13 = (bf16[256,256]{1,0:T(8,128)(2,1)S(1)}, bf16[256,256]{1,0:T(8,128)(2,1)S(1)}, u32[]{:S(2)}, u32[]{:S(2)}) collective-permute-start(bf16[256,256]{1,0:T(8,128)(2,1)S(1)} %collective-permute-done.12), channel_id=1, source_target_pairs={{0,2},{2,4},{4,6},{6,8},{8,10},{10,12},{12,14},{14,16},{16,18},{18... | collective-permute-start | bytes 393224 | tf_op jit(solution)/shard_map/ppermute | solution.py:86
  256.9 10.0 %collective-permute-start.14 = (bf16[256,256]{1,0:T(8,128)(2,1)S(1)}, bf16[256,256]{1,0:T(8,128)(2,1)S(1)}, u32[]{:S(2)}, u32[]{:S(2)}) collective-permute-start(bf16[256,256]{1,0:T(8,128)(2,1)S(1)} %collective-permute-done.13), channel_id=1, source_target_pairs={{0,2},{2,4},{4,6},{6,8},{8,10},{10,12},{12,14},{14,16},{16,18},{18... | collective-permute-start | bytes 393224 | tf_op jit(solution)/shard_map/ppermute | solution.py:86
  330.4 1.6 copy-start.3
  330.4 2.2 copy-start.4
  362.9 15.3 %copy-start.2 = (bf16[4096,256]{1,0:T(8,128)(2,1)S(1)}, bf16[4096,256]{1,0:T(8,128)(2,1)}, u32[]{:S(2)}) copy-start(bf16[4096,256]{1,0:T(8,128)(2,1)} %get-tuple-element.452) | copy-start | bytes 6291460 | tf_op jit(solution)/shard_map/while
  414.4 15.4 %copy-start.2 = (bf16[4096,256]{1,0:T(8,128)(2,1)S(1)}, bf16[4096,256]{1,0:T(8,128)(2,1)}, u32[]{:S(2)}) copy-start(bf16[4096,256]{1,0:T(8,128)(2,1)} %get-tuple-element.452) | copy-start | bytes 6291460 | tf_op jit(solution)/shard_map/while
  530.1 59.3 %copy-start.1 = (bf16[512,512]{1,0:T(8,128)(2,1)S(1)}, bf16[512,512]{1,0:T(8,128)(2,1)}, u32[]{:S(2)}) copy-start(bf16[512,512]{1,0:T(8,128)(2,1)} %param.15) | copy-start | bytes 1572868
Sparse Core Ops, SparseCore 0:
  9.5 53.0 all-gather.5
  64.8 48.8 all-gather.11
  115.3 187.2 all-gather.9
  304.6 40.1 all-gather.7
  346.2 167.1 all-gather.13
  530.2 54.3 reduce-scatter.1
